TPU v7x, 1024 devices: a whole 4x8x16 slice. The times are simulated.
1024 devices in a mesh: shard: 128 (over z, x, y_lo), rep: 8 (over y_hi, core).
Axes of the slice: x: 4, y: 8 (y_hi: 4, y_lo: 2; y = y_hi * 2 + y_lo), z: 16, core: 2. Of those that a mesh axis runs over, the one named last changes fastest.
Arguments:
- activations: bfloat16 [4, 65536, 2048], P(None, ('shard', 'rep')), may hold values from -24 to 24
- value_grad: bfloat16 [4, 65536, 512], P(None, ('shard', 'rep')), may hold values from -6 to 6
- norm_gain: bfloat16 [2048], P('shard'), may hold values from 0.25 to 4.5
- value_weight: bfloat16 [2048, 512], P('shard'), may hold values from -0.125 to 0.125
Outputs:
- input_grad: bfloat16 [4, 65536, 2048], P(None, ('shard', 'rep'))
- weight_update: float32 [2048, 512], P('shard')
All inputs are finite; a program needn't handle non-finite values.
Results may differ from a plain program's by a relative error of at most 0.0029.
Values may be sent and summed in bfloat16 or wider, within the bound.
A program may use at most 32 MiB of HBM per device.

v0:
```python
import functools
import math

import jax
import jax.numpy as jnp
from jax import lax
from jax.sharding import Mesh
from jax.sharding import PartitionSpec as P

SHARD = ("shard_0", "shard_1", "shard_2")
SHARD_REP = ("shard_0", "shard_1", "shard_2", "rep")


def sent_together(arrays, axis, dim, along):
    widths = [math.prod(a.shape[along:]) for a in arrays]
    both = jnp.concatenate(
        [a.reshape(*a.shape[:along], w) for a, w in zip(arrays, widths)], axis=along
    )
    whole = lax.all_gather(both, axis, axis=dim, tiled=True)
    parts = jnp.split(whole, [sum(widths[:k]) for k in range(1, len(widths))], axis=along)
    return tuple((b.reshape(*whole.shape[:along], *a.shape[along:]) for a, b in zip(arrays, parts)))


def sum_in_order(parts, axes, sequence):
    inside = parts.shape[1:]
    parts = parts.reshape(*(lax.axis_size(a) for a in axes), *inside)
    parts = jnp.moveaxis(parts, sequence, range(len(axes))).reshape(-1, *inside)
    for k in sequence:
        parts = lax.psum_scatter(parts, axes[k], scatter_dimension=0, tiled=True)
    return parts[0]


def split_up(array, dim, count):
    lengths = array.shape
    parts = array.reshape(*lengths[:dim], count, lengths[dim] // count, *lengths[dim + 1 :])
    return jnp.moveaxis(parts, dim, 0)


def summed_rows(array, axes, sequence, dim):
    count = lax.axis_size(axes)
    return sum_in_order(split_up(array, dim, count), axes, sequence)


def copy_for_each(array, axis):
    count = lax.axis_size(axis)
    return lax.all_to_all(
        jnp.broadcast_to(array[None], (count, *array.shape)), axis, 0, 0, tiled=True
    )


def taken_together(array, axis):
    everything = copy_for_each(array, axis)
    return jnp.sum(everything, axis=0)


def by_axis(array, axes):
    return functools.reduce(lax.psum, axes, array)


def on_device(activations, value_grad, norm_gain, value_weight):
    gain_all, weight_all = sent_together((norm_gain, value_weight), SHARD, 0, 1)
    gain = gain_all.astype(jnp.float32)
    width = activations.shape[2]
    columns = value_grad.shape[2]

    def one_batch(total, inputs):
        block, cotangent = inputs
        values = block.astype(jnp.float32)
        rstd = lax.rsqrt(jnp.mean(values * values, axis=-1, keepdims=True) + 1e-05)
        normed = (values * rstd * gain).astype(jnp.bfloat16)
        total = total + lax.dot_general(
            normed, cotangent, (((0,), (0,)), ((), ())), preferred_element_type=jnp.float32
        )
        normed_grad = jnp.dot(cotangent, weight_all.T, preferred_element_type=jnp.float32)
        scaled = normed_grad * gain
        inner = jnp.mean(scaled * values, axis=-1, keepdims=True)
        result = (rstd * scaled - values * rstd * rstd * rstd * inner).astype(jnp.bfloat16)
        return (total, result)

    start = jnp.zeros((width, columns), jnp.float32)
    grad_full, input_grad = lax.scan(one_batch, start, (activations, value_grad))
    partial_rows = summed_rows(grad_full, SHARD, (1, 0, 2), 0)
    summed = taken_together(partial_rows, "rep")
    squares = by_axis(jnp.sum(summed * summed), SHARD)
    factor = 1.0 / jnp.maximum(1.0, jnp.sqrt(squares / (width * columns)))
    return (input_grad, summed * factor)


def solution(mesh):
    split = Mesh(
        mesh.devices.reshape(16, 4, 2, mesh.shape["rep"]), ("shard_0", "shard_1", "shard_2", "rep")
    )
    placed = (P(None, SHARD_REP, None), P(None, SHARD_REP, None), P(SHARD), P(SHARD, None))
    return jax.shard_map(
        on_device,
        mesh=split,
        in_specs=placed,
        out_specs=(P(None, SHARD_REP, None), P(SHARD, None)),
        check_vma=False,
    )
```

profile of v0, /device:TPU:1, one launch (start us, length us, event | category | flops | bytes accessed | tf_op | source)
XLA Modules:
  0.0 870.0 jit_solution(1428826360302910853)
XLA Ops:
  7.2 0.0 copy-start.1
  7.2 0.0 copy-start
  7.2 0.0 all-gather.2.cloned.1.call-start
  7.2 0.8 copy.10
  8.1 1.4 pad_maximum_fusion
  9.5 0.0 all-gather.2.cloned.1.call-update
  9.5 0.0 reduce-scatter.4.cloned.1.call-start
  9.6 513.7 %all-gather.2.cloned.1.call-done = bf16[2048,513]{1,0:T(8,128)(2,1)} async-done(((bf16[16,513]{1,0:T(8,128)(2,1)}), bf16[2048,513]{1,0:T(8,128)(2,1)}) %all-gather.2.cloned.1.call-update) | async-done | bytes 2101264 | tf_op jit(solution)/shard_map/all_gather | solution.py:19
  523.3 1.3 convert_reduce_fusion
  524.6 2.8 split.9
  527.4 0.0 copy-done.1
  527.4 0.0 copy-done
  527.4 24.7 %while.13 = (s32[]{:T(128)}, f32[2048,512]{1,0:T(8,128)}, bf16[4,64,2048]{2,1,0:T(8,128)(2,1)}, bf16[4,64,2048]{2,1,0:T(8,128)(2,1)S(1)}, f32[2048]{0:T(1024)S(1...) while((s32[]{:T(128)}, f32[2048,512]{1,0:T(8,128)}, ...), condition=%wide.region_3.4_spmd.clone, body=%wide.region_0.3_spmd.clone.sunk | while | flops 272891968 | bytes 12735602 | solution.py:81
  527.4 0.9 fusion.34
  528.3 0.9 fusion.35
  529.2 2.7 select_add_fusion.2
  531.9 0.9 fusion.34
  532.8 0.9 fusion.35
  533.7 4.9 select_add_fusion.2
  538.6 0.9 fusion.34
  539.5 0.9 fusion.35
  540.4 4.9 select_add_fusion.2
  545.4 0.9 fusion.34
  546.2 0.9 fusion.35
  547.1 4.9 select_add_fusion.2
  552.1 5.0 copy.11
  557.1 0.0 reduce-scatter.4.cloned.1.call-update
  557.1 0.0 reduce-scatter.6.cloned.1.call-start
  557.1 145.5 %reduce-scatter.4.cloned.1.call-done = f32[32,16,512]{2,1,0:T(8,128)} async-done(((f32[128,16,512]{2,1,0:T(8,128)}), f32[32,16,512]{2,1,0:T(8,128)}) %reduce-scatter.4.cloned.1.call-update) | async-done | bytes 1048592 | tf_op jit(solution)/shard_map/reduce_scatter | solution.py:29
  702.6 0.0 reduce-scatter.6.cloned.1.call-update
  702.6 0.0 reduce-scatter.8.cloned.1.call-start
  702.7 68.3 %reduce-scatter.6.cloned.1.call-done = f32[2,16,512]{2,1,0:T(8,128)} async-done(((f32[32,16,512]{2,1,0:T(8,128)}), f32[2,16,512]{2,1,0:T(8,128)}) %reduce-scatter.6.cloned.1.call-update) | async-done | bytes 65552 | tf_op jit(solution)/shard_map/reduce_scatter | solution.py:29
  771.0 0.0 reduce-scatter.8.cloned.1.call-update
  771.1 33.1 %reduce-scatter.8.cloned.1.call-done = f32[1,16,512]{2,1,0:T(8,128)} async-done(((f32[2,16,512]{2,1,0:T(8,128)}), f32[1,16,512]{2,1,0:T(8,128)}) %reduce-scatter.8.cloned.1.call-update) | async-done | bytes 32784 | tf_op jit(solution)/shard_map/reduce_scatter | solution.py:29
  804.2 0.8 broadcast_in_dim.24
  805.0 16.9 %all_to_all.5 = f32[8,16,512]{2,1,0:T(8,128)S(1)} all-to-all(f32[8,16,512]{2,1,0:T(8,128)S(1)} %broadcast_in_dim.24), channel_id=1, replica_groups=mesh['shard_0'=16,'shard_1'=4,'shard_2'=2,'rep'=8] {'rep'}, dimensions={0} | all-to-all | bytes 524288 | tf_op jit(solution)/shard_map/all_to_all | solution.py:46
  821.9 0.6 multiply_reduce_fusion
  822.5 25.9 %psum.21 = f32[]{:T(128)} all-reduce(f32[]{:T(128)} %multiply_reduce_fusion), channel_id=1, replica_groups=mesh['shard_0'=16,'shard_1'=4,'shard_2'=2,'rep'=8] {'shard_0'}, use_global_device_ids=true, to_apply=%region_9.10 | all-reduce | flops 1 | bytes 8 | tf_op jit(solution)/shard_map/psum | solution.py:57
  848.4 9.3 %psum.22 = f32[]{:T(128)} all-reduce(f32[]{:T(128)} %psum.21), channel_id=1, replica_groups=mesh['shard_0'=16,'shard_1'=4,'shard_2'=2,'rep'=8] {'shard_1'}, use_global_device_ids=true, to_apply=%region_10.11 | all-reduce | flops 1 | bytes 8 | tf_op jit(solution)/shard_map/psum | solution.py:57
  857.7 4.4 psum.23
  862.9 0.6 broadcast_multiply_fusion.1
  (7 shorter events, 0.1 us)
Async XLA Ops:
  7.2 520.2 %copy-start.1 = (bf16[4,64,512]{2,1,0:T(8,128)(2,1)S(1)}, bf16[4,64,512]{2,1,0:T(8,128)(2,1)}, u32[]{:S(2)}) copy-start(bf16[4,64,512]{2,1,0:T(8,128)(2,1)} %param.7) | copy-start | bytes 786436
  7.2 520.2 %copy-start = (bf16[4,64,2048]{2,1,0:T(8,128)(2,1)S(1)}, bf16[4,64,2048]{2,1,0:T(8,128)(2,1)}, u32[]{:S(2)}) copy-start(bf16[4,64,2048]{2,1,0:T(8,128)(2,1)} %param.6) | copy-start | bytes 3145732
  7.2 516.1 %all-gather.2.cloned.1.call-start = ((), (), s32[]{:S(2)}) async-start(), calls=%async_computation.4 | async-start | bytes 2641920 | tf_op jit(solution)/shard_map/all_gather | solution.py:19
  9.5 693.1 %reduce-scatter.4.cloned.1.call-start = ((), (), s32[]{:S(2)}) async-start(), calls=%async_computation.5 | async-start | bytes 5242880 | tf_op jit(solution)/shard_map/reduce_scatter | solution.py:29
  557.1 213.9 %reduce-scatter.6.cloned.1.call-start = ((), (), s32[]{:S(2)}) async-start(), calls=%async_computation.6 | async-start | bytes 1114112 | tf_op jit(solution)/shard_map/reduce_scatter | solution.py:29
  702.6 101.6 %reduce-scatter.8.cloned.1.call-start = ((), (), s32[]{:S(2)}) async-start(), calls=%async_computation.7 | async-start | bytes 98304 | tf_op jit(solution)/shard_map/reduce_scatter | solution.py:29
Sparse Core Ops, SparseCore 0:
  11.2 512.0 all-gather.1
  557.2 145.3 reduce-scatter.3
  706.0 64.9 reduce-scatter.5
  774.2 29.9 reduce-scatter.7
where the time goes:
time: 881 us; the launch traced here: 870 us
  waiting for transfers between devices  761 us (86%)
  blocking collectives  56.5 us (6%)
  matrix products  21 us (2%)
  between operations  14.6 us (2%)
  local copies, waits for them, and re-layouts  9.42 us (1%)
    all_gather x1, waiting for transfers between devices, sent_together(): whole = lax.all_gather(both, axis, axis=dim, tiled=True)  514 us
    reduce_scatter x3, waiting for transfers between devices, sum_in_order(): parts = lax.psum_scatter(parts, axes[k], scatter_dimension=0, tiled=True)  247 us
    psum x3, blocking collectives, by_axis(): return functools.reduce(lax.psum, axes, array)  39.6 us
  transfers between devices with their start and end apart: 4, of which 4 were waited for; matrix products, arithmetic and copies ran while one was open for 0% of the time, Pallas kernels for 0%

commit v1 on v0

v1 whole, which is shorter than its diff:
```python
import functools

import jax
import jax.numpy as jnp
from jax import lax
from jax.experimental import pallas as pl
from jax.experimental.pallas import tpu as pltpu
from jax.sharding import Mesh
from jax.sharding import PartitionSpec as P

AXES = ("z", "x", "yl", "yh", "c")
NZ, NX, NYL, NYH, NC = 16, 4, 2, 4, 2
NY = NYL * NYH
MESH = pl.DeviceIdType.MESH
F32, BF16 = jnp.float32, jnp.bfloat16


def kernel(
    x_ref, vg_ref, w_ref, grow_ref, gcol_ref,
    out_ref, upd_ref,
    rstd, hi, lo, g, r, xs, xr, s, yr, s2, zr, gb, sq, sqz, sq2, sqx, wbuf, gbuf, hbuf, gainrow,
    wz_s, wz_r, gz_s, gz_r, wy_s, wy_r, gy_s, gy_r, wx_s, wx_r, gx_s, gx_r, wc_s, wc_r,
    dc_s, dc_r, rx_s, rx_r, ry_s, ry_r, rz_s, rz_r, rg_s, rg_r, qz_s, qz_r, qx_s, qx_r,
):
    iz, ix, il, ih, ic = (lax.axis_index(a) for a in AXES)
    iy = ih * NYL + il
    tokens, width = x_ref.shape
    oc = 1 - ic
    sends = []

    def at_x(k):
        return lax.rem(ix + k, NX)

    def at_y(k):
        return lax.rem(iy + k, NY)

    def at_z(k):
        return lax.rem(iz + k, NZ)

    def to_x(k):
        return {"x": at_x(k)}

    def to_y(k):
        y = at_y(k)
        return {"yh": y // NYL, "yl": lax.rem(y, NYL)}

    def to_z(k):
        return {"z": at_z(k)}

    def to_rep(k):
        return {"yh": lax.rem(ih + k // NC, NYH), "c": lax.rem(ic + k % NC, NC)}

    def to_plane(k):
        return {"x": at_x(k // NYL), "yl": lax.rem(il + k % NYL, NYL)}

    def send(src, dst, ss, rs, dev):
        copy = pltpu.make_async_remote_copy(
            src_ref=src, dst_ref=dst, send_sem=ss, recv_sem=rs, device_id=dev, device_id_type=MESH
        )
        copy.start()
        sends.append(copy)

    def arrived(dst, ss, rs):
        pltpu.make_async_remote_copy(
            src_ref=dst, dst_ref=dst, send_sem=ss, recv_sem=rs, device_id={"c": oc}, device_id_type=MESH
        ).wait_recv()

    barrier = pltpu.get_barrier_semaphore()
    peers = [to_z(k) for k in range(1, NZ)]
    peers += [to_y(k) for k in range(1, NY)]
    peers += [to_x(k) for k in range(1, NX)]
    peers += [to_plane(k) for k in range(1, NX * NYL) if k % NYL and k // NYL]
    peers += [to_rep(k) for k in range(1, NC * NYH) if k % NC]
    for dev in peers:
        pl.semaphore_signal(barrier, inc=1, device_id=dev, device_id_type=MESH)

    block = 32

    @pl.loop(0, tokens // block)
    def _(t):
        rows = pl.ds(pl.multiple_of(t * block, block), block)
        acc = jnp.zeros((block, 128), F32)
        for j in range(width // 128):
            v = x_ref[rows, j * 128 : (j + 1) * 128].astype(F32)
            acc = acc + v * v
        inv = lax.rsqrt(jnp.sum(acc, axis=1, keepdims=True) / width + 1e-05)
        rstd[rows, :] = jnp.broadcast_to(inv, (block, 128))
        scaled = vg_ref[rows, :].astype(F32) * inv
        high = scaled.astype(BF16)
        hi[rows, :] = high
        lo[rows, :] = (scaled - high.astype(F32)).astype(BF16)

    wbuf[ic, iz, ix, il] = w_ref[ic]
    gbuf[iz, ix, il] = grow_ref[...]
    pl.semaphore_wait(barrier, len(peers))

    for k in sorted(range(1, NZ), key=lambda k: -min(k, NZ - k)):
        send(w_ref.at[ic], wbuf.at[ic, iz, ix, il], wz_s.at[k - 1], wz_r.at[k - 1], to_z(k))
        send(grow_ref, gbuf.at[iz, ix, il], gz_s.at[k - 1], gz_r.at[k - 1], to_z(k))

    zs = 2
    feats = zs * 128

    @pl.loop(0, NZ // zs)
    def _(n):
        cols = pl.ds(pl.multiple_of(n * feats, feats), feats)
        xa = x_ref[:, cols]
        for half in range(2):
            hc = slice(half * 256, half * 256 + 256)
            dims = (((0,), (0,)), ((), ()))
            o = lax.dot_general(xa, hi[:, hc], dims, preferred_element_type=F32)
            o = o + lax.dot_general(xa, lo[:, hc], dims, preferred_element_type=F32)
            for zl in range(zs):
                for xx in range(NX):
                    for yl in range(NYL):
                        for cc in range(NC):
                            row = zl * 128 + xx * 32 + yl * 16 + cc * 8
                            for hh in range(2):
                                yy = (half * 2 + hh) * NYL + yl
                                at = pl.ds(pl.multiple_of(n * zs * 8 + zl * 8, 8), 8)
                                g[cc, xx, yy, at, :] = o[row : row + 8, hh * 128 : hh * 128 + 128]
        at = pl.ds(pl.multiple_of(n * zs * 8, 8), zs * 8)
        pltpu.make_async_remote_copy(
            src_ref=g.at[oc, :, :, at],
            dst_ref=r.at[:, :, at],
            send_sem=dc_s.at[n],
            recv_sem=dc_r.at[n],
            device_id={"c": oc},
            device_id_type=MESH,
        ).start()

    @pl.loop(0, NZ // zs)
    def _(n):
        at = pl.ds(pl.multiple_of(n * zs * 8, 8), zs * 8)
        pltpu.make_async_remote_copy(
            src_ref=g.at[oc, :, :, at],
            dst_ref=r.at[:, :, at],
            send_sem=dc_s.at[n],
            recv_sem=dc_r.at[n],
            device_id={"c": oc},
            device_id_type=MESH,
        ).wait()

    for k in (2, 1, 3):
        tx = at_x(k)

        @pl.loop(0, NY)
        def _(y):
            xs[k - 1, y] = (g[ic, tx, y] + r[tx, y]).astype(BF16)

        send(xs.at[k - 1], xr.at[k - 1], rx_s.at[k - 1], rx_r.at[k - 1], to_x(k))

    for k in range(1, NZ):
        fz = at_z(NZ - k)
        arrived(wbuf.at[ic, fz, ix, il], wz_s.at[k - 1], wz_r.at[k - 1])
        arrived(gbuf.at[fz, ix, il], gz_s.at[k - 1], gz_r.at[k - 1])
    send(wbuf.at[ic, :, ix, il], wbuf.at[ic, :, ix, il], wy_s, wy_r, {"yl": 1 - il})
    send(gbuf.at[:, ix, il], gbuf.at[:, ix, il], gy_s, gy_r, {"yl": 1 - il})

    for k in range(1, NX):
        arrived(xr.at[k - 1], rx_s.at[k - 1], rx_r.at[k - 1])

    def x_sum(y):
        total = g[ic, ix, y] + r[ix, y]
        for k in range(1, NX):
            total = total + xr[k - 1, y].astype(F32)
        return total

    for k in (4, 3, 5, 2, 6, 1, 7):
        y = at_y(k)
        s[y] = x_sum(y)
        send(s.at[y], yr.at[k - 1], ry_s.at[k - 1], ry_r.at[k - 1], to_y(k))
    s[iy] = x_sum(iy)

    arrived(wbuf.at[ic, :, ix, 1 - il], wy_s, wy_r)
    arrived(gbuf.at[:, ix, 1 - il], gy_s, gy_r)
    for k in (2, 1, 3):
        send(wbuf.at[ic, :, ix], wbuf.at[ic, :, ix], wx_s.at[k - 1], wx_r.at[k - 1], to_x(k))
        send(gbuf.at[:, ix], gbuf.at[:, ix], gx_s.at[k - 1], gx_r.at[k - 1], to_x(k))
    send(wbuf.at[ic, :, ix], wbuf.at[ic, :, ix], wc_s.at[0], wc_r.at[0], {"c": oc})

    total = s[iy]
    for k in range(1, NY):
        arrived(yr.at[k - 1], ry_s.at[k - 1], ry_r.at[k - 1])
        total = total + yr[k - 1]
    s2[...] = total

    for k in sorted(range(1, NZ), key=lambda k: -min(k, NZ - k)):
        at = pl.ds(pl.multiple_of(at_z(k) * 8, 8), 8)
        send(s2.at[at], zr.at[k - 1], rz_s.at[k - 1], rz_r.at[k - 1], to_z(k))

    for k in (1, 3, 2):
        fx = at_x(NX - k)
        arrived(wbuf.at[ic, :, fx], wx_s.at[k - 1], wx_r.at[k - 1])
        arrived(gbuf.at[:, fx], gx_s.at[k - 1], gx_r.at[k - 1])
        send(wbuf.at[ic, :, fx], wbuf.at[ic, :, fx], wc_s.at[k], wc_r.at[k], {"c": oc})
    for k in range(NX):
        fx = at_x(NX - k)
        arrived(wbuf.at[oc, :, fx], wc_s.at[k], wc_r.at[k])

    for z in range(NZ):
        row = jnp.zeros((1, 128), F32)
        for xx in range(NX):
            for yl in range(NYL):
                row = row + gbuf[z, xx, yl]
        gainrow[:, z * 128 : (z + 1) * 128] = jnp.broadcast_to(row, (8, 128))

    hbuf[:, width:] = jnp.zeros((tokens, 128), F32)

    @pl.loop(0, NZ)
    def _(z):
        cols = pl.ds(pl.multiple_of(z * 128, 128), 128)
        dims = (((1,), (1,)), ((), ()))
        h = jnp.zeros((tokens, 128), F32)
        for half in range(2):
            wt = wbuf[half, z].reshape(128, 256)
            h = h + lax.dot_general(
                vg_ref[:, half * 256 : half * 256 + 256], wt, dims, preferred_element_type=F32
            )
        h = h * gainrow[0:1, cols]
        hbuf[:, cols] = h
        hbuf[:, width:] += h * x_ref[:, cols].astype(F32)

    own = s2[pl.ds(pl.multiple_of(iz * 8, 8), 8), :]
    for k in range(1, NZ):
        arrived(zr.at[k - 1], rz_s.at[k - 1], rz_r.at[k - 1])
        own = own + zr[k - 1]
    gb[ih, ic] = own * gcol_ref[ic]
    for k in range(1, NYH * NC):
        send(gb.at[ih, ic], gb.at[ih, ic], rg_s.at[k - 1], rg_r.at[k - 1], to_rep(k))

    @pl.loop(0, tokens // block)
    def _(t):
        rows = pl.ds(pl.multiple_of(t * block, block), block)
        inner = jnp.sum(hbuf[rows, width:], axis=1, keepdims=True) / width
        inv = rstd[rows, 0:1]
        coef = inv * inv * inv * inner
        for j in range(width // 128):
            cs = slice(j * 128, (j + 1) * 128)
            v = x_ref[rows, cs].astype(F32)
            out_ref[rows, cs] = (inv * hbuf[rows, cs] - v * coef).astype(BF16)

    for k in range(1, NYH * NC):
        fh, fc = lax.rem(ih + NYH - k // NC, NYH), lax.rem(ic + k % NC, NC)
        arrived(gb.at[fh, fc], rg_s.at[k - 1], rg_r.at[k - 1])

    acc = jnp.zeros((8, 128), F32)
    for hh in range(NYH):
        for cc in range(NC):
            acc = acc + gb[hh, cc] * gb[hh, cc]
    sq[...] = acc
    for k in sorted(range(1, NZ), key=lambda k: -min(k, NZ - k)):
        send(sq, sqz.at[k - 1], qz_s.at[k - 1], qz_r.at[k - 1], to_z(k))
    for k in range(1, NZ):
        arrived(sqz.at[k - 1], qz_s.at[k - 1], qz_r.at[k - 1])
        acc = acc + sqz[k - 1]
    sq2[...] = acc
    for k in (5, 4, 3, 7, 2, 6, 1):
        send(sq2, sqx.at[k - 1], qx_s.at[k - 1], qx_r.at[k - 1], to_plane(k))
    for k in range(1, NX * NYL):
        arrived(sqx.at[k - 1], qx_s.at[k - 1], qx_r.at[k - 1])
        acc = acc + sqx[k - 1]
    squares = jnp.sum(jnp.sum(acc, axis=1, keepdims=True), axis=0, keepdims=True)
    factor = 1.0 / jnp.maximum(1.0, jnp.sqrt(squares / (width * 512)))
    for hh in range(NYH):
        for cc in range(NC):
            upd_ref[cc * 8 : cc * 8 + 8, hh * 128 : hh * 128 + 128] = gb[hh, cc] * factor

    for copy in sends:
        copy.wait_send()


def on_device(activations, value_grad, norm_gain, value_weight):
    batch, tok, width = activations.shape
    columns = value_grad.shape[2]
    tokens = batch * tok
    own = norm_gain.shape[0]
    gain = norm_gain.astype(F32)
    place = lax.axis_index("x") * NYL + lax.axis_index("yl")
    lanes = jnp.arange(128) // own == place
    grow = jnp.where(lanes, jnp.tile(gain, 128 // own), 0.0).reshape(1, 128)
    gcol = jnp.broadcast_to(gain.reshape(NC, own // NC, 1), (NC, own // NC, 128))
    weight = jnp.moveaxis(value_weight.reshape(own, NC, columns // NC), 1, 0)
    vm = pl.BlockSpec(memory_space=pltpu.VMEM)

    def dma(n):
        return pltpu.SemaphoreType.DMA((n,))

    def sem(n):
        return [dma(n), dma(n)]

    one = [pltpu.SemaphoreType.DMA, pltpu.SemaphoreType.DMA]
    v = pltpu.VMEM
    scratch = [
        v((tokens, 128), F32),
        v((tokens, columns), BF16),
        v((tokens, columns), BF16),
        v((NC, NX, NY, 128, 128), F32),
        v((NX, NY, 128, 128), F32),
        v((NX - 1, NY, 128, 128), BF16),
        v((NX - 1, NY, 128, 128), BF16),
        v((NY, 128, 128), F32),
        v((NY - 1, 128, 128), F32),
        v((128, 128), F32),
        v((NZ - 1, 8, 128), F32),
        v((NYH, NC, 8, 128), F32),
        v((8, 128), F32),
        v((NZ - 1, 8, 128), F32),
        v((8, 128), F32),
        v((NX * NYL - 1, 8, 128), F32),
        v((NC, NZ, NX, NYL, own, columns // NC), BF16),
        v((NZ, NX, NYL, 1, 128), F32),
        v((tokens, width + 128), F32),
        v((8, width), F32),
        *sem(NZ - 1), *sem(NZ - 1), *one, *one, *sem(NX - 1), *sem(NX - 1), *sem(NX),
        *sem(NZ // 2), *sem(NX - 1), *sem(NY - 1), *sem(NZ - 1), *sem(NYH * NC - 1), *sem(NZ - 1),
        *sem(NX * NYL - 1),
    ]
    result, update = pl.pallas_call(
        kernel,
        out_shape=(
            jax.ShapeDtypeStruct((tokens, width), BF16),
            jax.ShapeDtypeStruct((own, columns), F32),
        ),
        in_specs=[vm] * 5,
        out_specs=(vm, vm),
        scratch_shapes=scratch,
        compiler_params=pltpu.CompilerParams(
            collective_id=0, has_side_effects=True, vmem_limit_bytes=48 * 1024 * 1024
        ),
        name="normed_value_backward",
    )(activations.reshape(tokens, width), value_grad.reshape(tokens, columns), weight, grow, gcol)
    return result.reshape(activations.shape), update


def solution(mesh):
    split = Mesh(mesh.devices.reshape(NZ, NX, NYL, NYH, NC), AXES)
    rows = ("z", "x", "yl")
    placed = (P(None, AXES, None), P(None, AXES, None), P(rows), P(rows, None))
    return jax.shard_map(
        on_device,
        mesh=split,
        in_specs=placed,
        out_specs=(P(None, AXES, None), P(rows, None)),
        check_vma=False,
    )
```

time: 881 us -> 85.8 us (0.10); the launches traced: 870 us -> 84.1 us
  waiting for transfers between devices: 761 us -> 0 us
  Pallas kernels: 0 us -> 78.8 us
  blocking collectives: 56.5 us -> 0 us
  matrix products: 21 us -> 0 us
  between operations: 14.6 us -> 0.67 us
    all_gather x1 -> x0, waiting for transfers between devices: 514 us -> none  [sent_together(): whole = lax.all_gather(both, axis, axis=dim, tiled=True)]
    reduce_scatter x3 -> x0, waiting for transfers between devices: 247 us -> none  [sum_in_order(): parts = lax.psum_scatter(parts, axes[k], scatter_dimension=0, tiled=True)]
    pallas_call x0 -> x1, Pallas kernels: none -> 78.8 us  [on_device(): pl.pallas_call(kernel, out_shape=(jax.ShapeDtypeStruct((tokens, width), B...]
    psum x3 -> x0, blocking collectives: 39.6 us -> none  [by_axis(): return functools.reduce(lax.psum, axes, array)]
    dot_general x8 -> x0, matrix products: 21 us -> none  [the longest x4 17.6 us: one_batch(): lax.dot_general(normed, cotangent, (((0,), (0,)), ((), ())), preferred_el...]
    all_to_all x1 -> x0, blocking collectives: 16.9 us -> none  [copy_for_each(): lax.all_to_all(jnp.broadcast_to(array[None], (count, *array.shape)), axis...]
  transfers between devices with their start and end apart: 4 -> 0, of which waited for: 4 -> 0; matrix products, arithmetic and copies ran while one was open for 0% -> 0% of each run, Pallas kernels for 0% -> 0%
where the time goes in v1:
time: 85.8 us; the launch traced here: 84.1 us
  Pallas kernels  78.8 us (92%)
  local copies, waits for them, and re-layouts  4.64 us (5%)
    pallas_call x1, Pallas kernels, on_device(): pl.pallas_call(kernel, out_shape=(jax.ShapeDtypeStruct((tokens, width), B...  78.8 us
    unnamed x10, local copies, waits for them, and re-layouts  4.41 us

profile of v1, /device:TPU:1, one launch (start us, length us, event | category | flops | bytes accessed | tf_op | source)
XLA Modules:
  0.0 84.1 jit_solution(10168884476917840777)
XLA Ops:
  0.6 0.0 copy-start.3
  0.6 0.0 copy-start.2
  0.7 0.6 copy-done.3
  1.3 0.1 broadcast_in_dim.12
  1.4 0.1 tile.10
  1.5 0.1 broadcast_in_dim.13.gcol_ref
  1.5 0.0 copy-done.2
  1.5 0.0 copy-start
  1.5 1.2 %copy-done = bf16[4,64,2048]{2,1,0:T(8,128)(2,1)S(1)} copy-done((bf16[4,64,2048]{2,1,0:T(8,128)(2,1)S(1)}, bf16[4,64,2048]{2,1,0:T(8,128)(2,1)}, u32[]{:S(2)}) %copy-start) | copy-done | bytes 1048600
  2.8 0.0 copy-start.1
  2.8 0.9 %copy-done.1 = bf16[4,64,512]{2,1,0:T(8,128)(2,1)S(1)} copy-done((bf16[4,64,512]{2,1,0:T(8,128)(2,1)S(1)}, bf16[4,64,512]{2,1,0:T(8,128)(2,1)}, u32[]{:S(2)}) %copy-start.1) | copy-done | bytes 262168
  3.7 78.8 %normed_value_backward.1 = (bf16[256,2048]{1,0:T(8,128)(2,1)S(1)}, f32[16,512]{1,0:T(8,128)S(1)}) custom-call(bf16[256,2048]{1,0:T(8,128)(2,1)S(1)} %bitcast.10, bf16[256,512]{1,0:T(8,128)(2,1)S(1)} %bitcast.12, bf16[2,16,256]{2,1,0:T(8,128)(2,1)S(1)} %bitcast.13, f32[1,128]{1,0:T(1,128)S(1)} %compare_select_fusion.grow_ref, ...), custom_call_target="tpu_custom_call" | custom-call | tf_op jit(solution)/shard_map/normed_value_backward/pallas_call | solution.py:319
  82.5 1.0 %copy.12 = bf16[4,64,2048]{2,1,0:T(8,128)(2,1)} copy(bf16[4,64,2048]{2,1,0:T(8,128)(2,1)S(1)} %bitcast.11) | data formatting | bytes 2097152
  83.5 0.6 copy.13
  (3 shorter events, 0.0 us)
Async XLA Ops:
  0.6 0.7 copy-start.3
  0.6 0.9 %copy-start.2 = (bf16[16,512]{1,0:T(8,128)(2,1)S(1)}, bf16[16,512]{1,0:T(8,128)(2,1)}, u32[]{:S(2)}) copy-start(bf16[16,512]{1,0:T(8,128)(2,1)} %param.7) | copy-start | bytes 49156
  1.5 1.2 %copy-start = (bf16[4,64,2048]{2,1,0:T(8,128)(2,1)S(1)}, bf16[4,64,2048]{2,1,0:T(8,128)(2,1)}, u32[]{:S(2)}) copy-start(bf16[4,64,2048]{2,1,0:T(8,128)(2,1)} %param.4) | copy-start | bytes 3145732
  2.8 0.9 %copy-start.1 = (bf16[4,64,512]{2,1,0:T(8,128)(2,1)S(1)}, bf16[4,64,512]{2,1,0:T(8,128)(2,1)}, u32[]{:S(2)}) copy-start(bf16[4,64,512]{2,1,0:T(8,128)(2,1)} %param.5) | copy-start | bytes 786436

commit v2 on v1

v2 whole, which is shorter than its diff:
```python
import jax
import jax.numpy as jnp
from jax import lax
from jax.experimental import pallas as pl
from jax.experimental.pallas import tpu as pltpu
from jax.sharding import Mesh
from jax.sharding import PartitionSpec as P

AXES = ("z", "x", "yl", "yh", "c")
NZ, NX, NYL, NYH, NC = 16, 4, 2, 4, 2
NY = NYL * NYH
NG = NZ // 2
FAR = (4, 3, 5)
NEAR = (2, 6, 1, 7)
MESH = pl.DeviceIdType.MESH
F32, BF16 = jnp.float32, jnp.bfloat16


def kernel(
    x_hbm, vg_hbm, w_ref, grow_ref, gcol_ref,
    out_ref, upd_ref,
    x_ref, vg_ref, rstd, hi, lo, g, r, xs, xr, s, sb, yr, yb, s2, zr, gb, sqp, sqz,
    wbuf, gbuf, hbuf, gainrow,
    ld, wz_s, wz_r, gz_s, gz_r, wy_s, wy_r, gy_s, gy_r, wx_s, wx_r, gx_s, gx_r, wc_s, wc_r,
    dc_s, dc_r, rx_s, rx_r, ry_s, ry_r, rz_s, rz_r, rg_s, rg_r, qp_s, qp_r, qz_s, qz_r,
):
    iz, ix, il, ih, ic = (lax.axis_index(a) for a in AXES)
    iy = ih * NYL + il
    parity = lax.rem(iz, 2)
    tokens, width = x_ref.shape
    oc = 1 - ic
    sibling = {"c": oc}
    sends = []

    def at_x(k):
        return lax.rem(ix + k, NX)

    def at_y(k):
        return lax.rem(iy + k, NY)

    def at_z(k):
        return lax.rem(iz + k, NZ)

    def to_x(k):
        return {"x": at_x(k)}

    def to_y(k):
        y = at_y(k)
        return {"yh": y // NYL, "yl": lax.rem(y, NYL)}

    def to_rep(k):
        return {"yh": lax.rem(ih + k // NC, NYH), "c": lax.rem(ic + k % NC, NC)}

    def to_plane(k):
        return {"x": at_x(k // NY), **to_y(k % NY)}

    def to_column(k):
        return {"z": at_z(k // NC), "c": lax.rem(ic + k % NC, NC)}

    def remote(src, dst, ss, rs, dev):
        return pltpu.make_async_remote_copy(
            src_ref=src, dst_ref=dst, send_sem=ss, recv_sem=rs, device_id=dev, device_id_type=MESH
        )

    def send(*args):
        copy = remote(*args)
        copy.start()
        sends.append(copy)

    def arrived(dst, ss, rs):
        remote(dst, dst, ss, rs, sibling).wait_recv()

    barrier = pltpu.get_barrier_semaphore()
    peers = [to_column(k) for k in range(1, NZ * NC)]
    peers += [to_plane(k) for k in range(1, NX * NY)]
    peers += [to_rep(k) for k in range(1, NYH * NC) if k % NC and k // NC]
    for dev in peers:
        pl.semaphore_signal(barrier, inc=1, device_id=dev, device_id_type=MESH)

    parts = ld.shape[0] - 1
    chunk = tokens // parts
    loads = [
        pltpu.make_async_copy(
            x_hbm.at[pl.ds(t * chunk, chunk)], x_ref.at[pl.ds(t * chunk, chunk)], ld.at[t]
        )
        for t in range(parts)
    ]
    loads.append(pltpu.make_async_copy(vg_hbm, vg_ref, ld.at[parts]))
    for t in (0, parts, *range(1, parts)):
        loads[t].start()
    wbuf[ic, iz, ix, il] = w_ref[ic]
    gbuf[iz, ix, il] = grow_ref[...]

    block = 32
    for t in range(parts):
        loads[t].wait()
        if t == 0:
            loads[parts].wait()

        @pl.loop(t * chunk // block, (t + 1) * chunk // block)
        def _(b):
            rows = pl.ds(pl.multiple_of(b * block, block), block)
            acc = jnp.zeros((block, 128), F32)
            for j in range(width // 128):
                v = x_ref[rows, j * 128 : (j + 1) * 128].astype(F32)
                acc = acc + v * v
            inv = lax.rsqrt(jnp.sum(acc, axis=1, keepdims=True) / width + 1e-05)
            rstd[rows, :] = jnp.broadcast_to(inv, (block, 128))
            scaled = vg_ref[rows, :].astype(F32) * inv
            high = scaled.astype(BF16)
            hi[rows, :] = high
            lo[rows, :] = (scaled - high.astype(F32)).astype(BF16)

    def group(n):
        half = (n + 1) // 2
        return lax.rem(iz // 2 + NG // 2 + half * (1 - 2 * (n % 2)), NG)

    def gradient(n):
        cols = pl.ds(pl.multiple_of(group(n) * 256, 256), 256)
        xa = x_ref[:, cols]
        for half in range(2):
            hc = slice(half * 256, half * 256 + 256)
            dims = (((0,), (0,)), ((), ()))
            o = lax.dot_general(xa, hi[:, hc], dims, preferred_element_type=F32)
            o = o + lax.dot_general(xa, lo[:, hc], dims, preferred_element_type=F32)
            for zl in range(2):
                for xx in range(NX):
                    for yl in range(NYL):
                        for cc in range(NC):
                            row = zl * 128 + xx * 32 + yl * 16 + cc * 8
                            for hh in range(2):
                                yy = (half * 2 + hh) * NYL + yl
                                g[cc, n, xx, yy, zl * 8 : zl * 8 + 8, :] = o[
                                    row : row + 8, hh * 128 : hh * 128 + 128
                                ]

    def core_copy(n):
        return remote(g.at[oc, n], r.at[n], dc_s.at[n], dc_r.at[n], sibling)

    def x_copy(k, n):
        return remote(
            xs.at[k - 1, n], xr.at[k - 1, n], rx_s.at[k - 1, n], rx_r.at[k - 1, n], to_x(k)
        )

    def y_copy(k, n):
        y = at_y(k)
        if k in FAR:
            j = FAR.index(k)
            src, dst = sb.at[j, n], yb.at[j, n]
        else:
            src, dst = s.at[n, y], yr.at[NEAR.index(k), n]
        return remote(src, dst, ry_s.at[k - 1, n], ry_r.at[k - 1, n], to_y(k))

    def z_copy(zl, n):
        rows = pl.ds(pl.multiple_of(zl * 8, 8), 8)
        return remote(
            s2.at[n, rows], zr.at[iz], rz_s.at[n, zl], rz_r.at[iz], {"z": group(n) * 2 + zl}
        )

    def reduce_x(n):
        core_copy(n).wait_recv()
        for k in (2, 1, 3):
            tx = at_x(k)
            xs[k - 1, n] = (g[ic, n, tx] + r[n, tx]).astype(BF16)
            x_copy(k, n).start()

    def reduce_y(n):
        for k in range(1, NX):
            x_copy(k, n).wait_recv()
        total = g[ic, n, ix] + r[n, ix]
        for k in range(1, NX):
            total = total + xr[k - 1, n].astype(F32)
        s[n] = total
        for j, k in enumerate(FAR):
            sb[j, n] = s[n, at_y(k)].astype(BF16)
        for k in FAR + NEAR:
            y_copy(k, n).start()

    def reduce_z(n):
        total = s[n, iy]
        for k in FAR + NEAR:
            y_copy(k, n).wait_recv()
            total = total + (
                yb[FAR.index(k), n].astype(F32) if k in FAR else yr[NEAR.index(k), n]
            )
        s2[n] = total

    gradient(0)
    gradient(1)
    pl.semaphore_wait(barrier, len(peers))
    core_copy(0).start()
    core_copy(1).start()

    for k in sorted(range(1, NZ), key=lambda k: -min(k, NZ - k)):
        dev = {"z": at_z(k)}
        send(w_ref.at[ic], wbuf.at[ic, iz, ix, il], wz_s.at[k - 1], wz_r.at[k - 1], dev)
        send(grow_ref, gbuf.at[iz, ix, il], gz_s.at[k - 1], gz_r.at[k - 1], dev)

    lag = 3

    @pl.loop(2, NG)
    def _(n):
        gradient(n)
        core_copy(n).start()

        @pl.when(n >= lag)
        def _():
            reduce_x(n - lag)

    @pl.loop(NG - lag, NG)
    def _(n):
        reduce_x(n)

    @pl.loop(0, 3)
    def _(n):
        reduce_y(n)

    for k in range(1, NZ):
        fz = at_z(NZ - k)
        arrived(wbuf.at[ic, fz, ix, il], wz_s.at[k - 1], wz_r.at[k - 1])
        arrived(gbuf.at[fz, ix, il], gz_s.at[k - 1], gz_r.at[k - 1])
    send(wbuf.at[ic, :, ix, il], wbuf.at[ic, :, ix, il], wy_s, wy_r, {"yl": 1 - il})
    send(gbuf.at[:, ix, il], gbuf.at[:, ix, il], gy_s, gy_r, {"yl": 1 - il})

    behind = 3

    @pl.loop(3, NG)
    def _(n):
        reduce_y(n)
        reduce_z(n - behind)
        for zl in range(2):
            z_copy(zl, n - behind).start()

    arrived(wbuf.at[ic, :, ix, 1 - il], wy_s, wy_r)
    arrived(gbuf.at[:, ix, 1 - il], gy_s, gy_r)
    for k in (2, 1, 3):
        send(wbuf.at[ic, :, ix], wbuf.at[ic, :, ix], wx_s.at[k - 1], wx_r.at[k - 1], to_x(k))
        send(gbuf.at[:, ix], gbuf.at[:, ix], gx_s.at[k - 1], gx_r.at[k - 1], to_x(k))
    send(wbuf.at[ic, :, ix], wbuf.at[ic, :, ix], wc_s.at[0], wc_r.at[0], sibling)

    @pl.loop(NG - behind, NG - 1)
    def _(n):
        reduce_z(n)
        for zl in range(2):
            z_copy(zl, n).start()

    reduce_z(NG - 1)
    z_copy(1 - parity, NG - 1).start()

    own = s2[NG - 1, pl.ds(pl.multiple_of(parity * 8, 8), 8), :]
    for k in sorted(range(1, NZ), key=lambda k: -min(k, NZ - k)):
        fz = at_z(k)
        arrived(zr.at[fz], rz_s.at[0, 0], rz_r.at[fz])
        own = own + zr[fz]
    piece = own * gcol_ref[ic]
    gb[ih, ic] = piece
    here = ix * NY + iy
    sqp[here] = jnp.sum(piece * piece, axis=0, keepdims=True)
    for k in sorted(range(1, NX * NY), key=lambda k: -min(k % NY, NY - k % NY)):
        send(sqp.at[here], sqp.at[here], qp_s.at[k - 1], qp_r.at[here], to_plane(k))
    for k in range(1, NYH * NC):
        send(gb.at[ih, ic], gb.at[ih, ic], rg_s.at[k - 1], rg_r.at[k - 1], to_rep(k))
    for k in range(1, NX * NY):
        there = at_x(k // NY) * NY + at_y(k % NY)
        arrived(sqp.at[there], qp_s.at[0], qp_r.at[there])
    row = sqp[0]
    for k in range(1, NX * NY):
        row = row + sqp[k]

    there = iz * NC + ic
    sqz[there] = row
    for k in sorted(range(1, NZ * NC), key=lambda k: -min(k // NC, NZ - k // NC)):
        send(sqz.at[there], sqz.at[there], qz_s.at[k - 1], qz_r.at[there], to_column(k))

    for k in (1, 3, 2):
        fx = at_x(NX - k)
        arrived(wbuf.at[ic, :, fx], wx_s.at[k - 1], wx_r.at[k - 1])
        arrived(gbuf.at[:, fx], gx_s.at[k - 1], gx_r.at[k - 1])
        send(wbuf.at[ic, :, fx], wbuf.at[ic, :, fx], wc_s.at[k], wc_r.at[k], sibling)
    for z in range(NZ):
        row = jnp.zeros((1, 128), F32)
        for xx in range(NX):
            for yl in range(NYL):
                row = row + gbuf[z, xx, yl]
        gainrow[:, z * 128 : (z + 1) * 128] = jnp.broadcast_to(row, (8, 128))
    hbuf[:, width:] = jnp.zeros((tokens, 128), F32)
    for k in range(NX):
        fx = at_x(NX - k)
        arrived(wbuf.at[oc, :, fx], wc_s.at[k], wc_r.at[k])

    @pl.loop(0, NG)
    def _(n):
        cols = pl.ds(pl.multiple_of(n * 256, 256), 256)
        dims = (((1,), (1,)), ((), ()))
        h = jnp.zeros((tokens, 256), F32)
        for half in range(2):
            wt = wbuf[half, pl.ds(n * 2, 2)].reshape(256, 256)
            h = h + lax.dot_general(
                vg_ref[:, half * 256 : half * 256 + 256], wt, dims, preferred_element_type=F32
            )
        h = h * gainrow[0:1, cols]
        hbuf[:, cols] = h
        hx = h * x_ref[:, cols].astype(F32)
        hbuf[:, width:] += hx[:, :128] + hx[:, 128:]

    @pl.loop(0, tokens // block)
    def _(t):
        rows = pl.ds(pl.multiple_of(t * block, block), block)
        inner = jnp.sum(hbuf[rows, width:], axis=1, keepdims=True) / width
        inv = rstd[rows, 0:1]
        coef = inv * inv * inv * inner
        for j in range(width // 128):
            cs = slice(j * 128, (j + 1) * 128)
            v = x_ref[rows, cs].astype(F32)
            out_ref[rows, cs] = (inv * hbuf[rows, cs] - v * coef).astype(BF16)

    for k in range(1, NYH * NC):
        fh, fc = lax.rem(ih + NYH - k // NC, NYH), lax.rem(ic + k % NC, NC)
        arrived(gb.at[fh, fc], rg_s.at[k - 1], rg_r.at[k - 1])
    for k in range(1, NZ * NC):
        there = at_z(k // NC) * NC + lax.rem(ic + k % NC, NC)
        arrived(sqz.at[there], qz_s.at[0], qz_r.at[there])
    row = sqz[0]
    for k in range(1, NZ * NC):
        row = row + sqz[k]
    squares = jnp.sum(row, axis=1, keepdims=True)
    factor = 1.0 / jnp.maximum(1.0, jnp.sqrt(squares / (width * 512)))
    for hh in range(NYH):
        for cc in range(NC):
            upd_ref[cc * 8 : cc * 8 + 8, hh * 128 : hh * 128 + 128] = gb[hh, cc] * factor

    for copy in sends:
        copy.wait_send()

    @pl.loop(0, NG)
    def _(n):
        core_copy(n).wait_send()
        for k in range(1, NX):
            x_copy(k, n).wait_send()
        for k in range(1, NY):
            y_copy(k, n).wait_send()

    @pl.loop(0, NG - 1)
    def _(n):
        for zl in range(2):
            z_copy(zl, n).wait_send()

    z_copy(1 - parity, NG - 1).wait_send()


def on_device(activations, value_grad, norm_gain, value_weight):
    batch, tok, width = activations.shape
    columns = value_grad.shape[2]
    tokens = batch * tok
    own = norm_gain.shape[0]
    gain = norm_gain.astype(F32)
    place = lax.axis_index("x") * NYL + lax.axis_index("yl")
    lanes = jnp.arange(128) // own == place
    grow = jnp.where(lanes, jnp.tile(gain, 128 // own), 0.0).reshape(1, 128)
    gcol = jnp.broadcast_to(gain.reshape(NC, own // NC, 1), (NC, own // NC, 128))
    weight = jnp.moveaxis(value_weight.reshape(own, NC, columns // NC), 1, 0)
    vm = pl.BlockSpec(memory_space=pltpu.VMEM)
    hbm = pl.BlockSpec(memory_space=pltpu.HBM)
    dma = pltpu.SemaphoreType.DMA

    def sem(*n):
        kind = dma(n) if n else dma
        return [kind, kind]

    v = pltpu.VMEM
    scratch = [
        v((tokens, width), BF16),
        v((tokens, columns), BF16),
        v((tokens, 128), F32),
        v((tokens, columns), BF16),
        v((tokens, columns), BF16),
        v((NC, NG, NX, NY, 16, 128), F32),
        v((NG, NX, NY, 16, 128), F32),
        v((NX - 1, NG, NY, 16, 128), BF16),
        v((NX - 1, NG, NY, 16, 128), BF16),
        v((NG, NY, 16, 128), F32),
        v((len(FAR), NG, 16, 128), BF16),
        v((len(NEAR), NG, 16, 128), F32),
        v((len(FAR), NG, 16, 128), BF16),
        v((NG, 16, 128), F32),
        v((NZ, 8, 128), F32),
        v((NYH, NC, 8, 128), F32),
        v((NX * NY, 1, 128), F32),
        v((NZ * NC, 1, 128), F32),
        v((NC, NZ, NX, NYL, own, columns // NC), BF16),
        v((NZ, NX, NYL, 1, 128), F32),
        v((tokens, width + 128), F32),
        v((8, width), F32),
        dma((5,)),
        *sem(NZ - 1), *sem(NZ - 1), *sem(), *sem(), *sem(NX - 1), *sem(NX - 1), *sem(NX),
        *sem(NG), *sem(NX - 1, NG), *sem(NY - 1, NG), dma((NG, 2)), dma((NZ,)),
        *sem(NYH * NC - 1), dma((NX * NY - 1,)), dma((NX * NY,)),
        dma((NZ * NC - 1,)), dma((NZ * NC,)),
    ]
    result, update = pl.pallas_call(
        kernel,
        out_shape=(
            jax.ShapeDtypeStruct((tokens, width), BF16),
            jax.ShapeDtypeStruct((own, columns), F32),
        ),
        in_specs=[hbm, hbm, vm, vm, vm],
        out_specs=(vm, vm),
        scratch_shapes=scratch,
        compiler_params=pltpu.CompilerParams(
            collective_id=0, has_side_effects=True, vmem_limit_bytes=48 * 1024 * 1024
        ),
        name="normed_value_backward",
    )(activations.reshape(tokens, width), value_grad.reshape(tokens, columns), weight, grow, gcol)
    return result.reshape(activations.shape), update


def solution(mesh):
    split = Mesh(mesh.devices.reshape(NZ, NX, NYL, NYH, NC), AXES)
    rows = ("z", "x", "yl")
    placed = (P(None, AXES, None), P(None, AXES, None), P(rows), P(rows, None))
    return jax.shard_map(
        on_device,
        mesh=split,
        in_specs=placed,
        out_specs=(P(None, AXES, None), P(rows, None)),
        check_vma=False,
    )
```

time: 85.8 us -> 74.3 us (0.87); the launches traced: 84.1 us -> 74.1 us
  Pallas kernels: 78.8 us -> 68.7 us
    pallas_call x1, Pallas kernels: 78.8 us -> 68.7 us  [on_device(): pl.pallas_call(kernel, out_shape=(jax.ShapeDtypeStruct((tokens, width), B...]
where the time goes in v2:
time: 74.3 us; the launch traced here: 74.1 us
  Pallas kernels  68.7 us (92%)
  local copies, waits for them, and re-layouts  4.64 us (6%)
    pallas_call x1, Pallas kernels, on_device(): pl.pallas_call(kernel, out_shape=(jax.ShapeDtypeStruct((tokens, width), B...  68.7 us
    unnamed x10, local copies, waits for them, and re-layouts  4.41 us

profile of v2, /device:TPU:1, one launch (start us, length us, event | category | flops | bytes accessed | tf_op | source)
XLA Modules:
  0.0 74.1 jit_solution(917800074873294110)
XLA Ops:
  0.6 0.0 copy-start.3
  0.6 0.0 copy-start.2
  0.7 0.6 copy-done.3
  1.3 0.1 broadcast_in_dim.12
  1.4 0.1 tile.10
  1.5 0.1 broadcast_in_dim.13.gcol_ref
  1.5 0.0 copy-done.2
  1.5 0.0 copy-start
  1.5 1.2 %copy-done = bf16[4,64,2048]{2,1,0:T(8,128)(2,1)S(1)} copy-done((bf16[4,64,2048]{2,1,0:T(8,128)(2,1)S(1)}, bf16[4,64,2048]{2,1,0:T(8,128)(2,1)}, u32[]{:S(2)}) %copy-start) | copy-done | bytes 1048600
  2.8 0.0 copy-start.1
  2.8 0.9 %copy-done.1 = bf16[4,64,512]{2,1,0:T(8,128)(2,1)S(1)} copy-done((bf16[4,64,512]{2,1,0:T(8,128)(2,1)S(1)}, bf16[4,64,512]{2,1,0:T(8,128)(2,1)}, u32[]{:S(2)}) %copy-start.1) | copy-done | bytes 262168
  3.7 68.7 %normed_value_backward.1 = (bf16[256,2048]{1,0:T(8,128)(2,1)S(1)}, f32[16,512]{1,0:T(8,128)S(1)}) custom-call(bf16[256,2048]{1,0:T(8,128)(2,1)S(1)} %bitcast.10, bf16[256,512]{1,0:T(8,128)(2,1)S(1)} %bitcast.12, bf16[2,16,256]{2,1,0:T(8,128)(2,1)S(1)} %bitcast.13, f32[1,128]{1,0:T(1,128)S(1)} %compare_select_fusion.grow_ref, ...), custom_call_target="tpu_custom_call" | custom-call | tf_op jit(solution)/shard_map/normed_value_backward/pallas_call | solution.py:400
  72.5 1.0 %copy.12 = bf16[4,64,2048]{2,1,0:T(8,128)(2,1)} copy(bf16[4,64,2048]{2,1,0:T(8,128)(2,1)S(1)} %bitcast.11) | data formatting | bytes 2097152
  73.4 0.6 copy.13
  (3 shorter events, 0.0 us)
Async XLA Ops:
  0.6 0.7 copy-start.3
  0.6 0.9 %copy-start.2 = (bf16[16,512]{1,0:T(8,128)(2,1)S(1)}, bf16[16,512]{1,0:T(8,128)(2,1)}, u32[]{:S(2)}) copy-start(bf16[16,512]{1,0:T(8,128)(2,1)} %param.7) | copy-start | bytes 49156
  1.5 1.2 %copy-start = (bf16[4,64,2048]{2,1,0:T(8,128)(2,1)S(1)}, bf16[4,64,2048]{2,1,0:T(8,128)(2,1)}, u32[]{:S(2)}) copy-start(bf16[4,64,2048]{2,1,0:T(8,128)(2,1)} %param.4) | copy-start | bytes 3145732
  2.8 0.9 %copy-start.1 = (bf16[4,64,512]{2,1,0:T(8,128)(2,1)S(1)}, bf16[4,64,512]{2,1,0:T(8,128)(2,1)}, u32[]{:S(2)}) copy-start(bf16[4,64,512]{2,1,0:T(8,128)(2,1)} %param.5) | copy-start | bytes 786436

commit v3 on v2

--- a/solution.py
+++ b/solution.py
@@ -17,9 +17,9 @@
 
 
 def kernel(
-    x_hbm, vg_hbm, w_ref, grow_ref, gcol_ref,
+    x_hbm, vg_hbm, gain_hbm, w_hbm,
     out_ref, upd_ref,
-    x_ref, vg_ref, rstd, hi, lo, g, r, xs, xr, s, sb, yr, yb, s2, zr, gb, sqp, sqz,
+    x_ref, vg_ref, w_ref, gain_ref, grow_ref, gcol_ref, rstd, hi, lo, g, r, xs, xr, s, sb, yr, yb, s2, zr, gb, sqp, sqz,
     wbuf, gbuf, hbuf, gainrow,
     ld, wz_s, wz_r, gz_s, gz_r, wy_s, wy_r, gy_s, gy_r, wx_s, wx_r, gx_s, gx_r, wc_s, wc_r,
     dc_s, dc_r, rx_s, rx_r, ry_s, ry_r, rz_s, rz_r, rg_s, rg_r, qp_s, qp_r, qz_s, qz_r,
@@ -70,14 +70,7 @@
     def arrived(dst, ss, rs):
         remote(dst, dst, ss, rs, sibling).wait_recv()
 
-    barrier = pltpu.get_barrier_semaphore()
-    peers = [to_column(k) for k in range(1, NZ * NC)]
-    peers += [to_plane(k) for k in range(1, NX * NY)]
-    peers += [to_rep(k) for k in range(1, NYH * NC) if k % NC and k // NC]
-    for dev in peers:
-        pl.semaphore_signal(barrier, inc=1, device_id=dev, device_id_type=MESH)
-
-    parts = ld.shape[0] - 1
+    parts = ld.shape[0] - 4
     chunk = tokens // parts
     loads = [
         pltpu.make_async_copy(
@@ -86,12 +79,24 @@
         for t in range(parts)
     ]
     loads.append(pltpu.make_async_copy(vg_hbm, vg_ref, ld.at[parts]))
-    for t in (0, parts, *range(1, parts)):
+    for h in range(NC):
+        cols = pl.ds(h * w_ref.shape[2], w_ref.shape[2])
+        loads.append(
+            pltpu.make_async_copy(w_hbm.at[:, cols], w_ref.at[h], ld.at[parts + 1 + h])
+        )
+    loads.append(pltpu.make_async_copy(gain_hbm, gain_ref, ld.at[parts + 3]))
+    for t in (0, parts, *range(1, parts), *range(parts + 1, parts + 4)):
         loads[t].start()
-    wbuf[ic, iz, ix, il] = w_ref[ic]
-    gbuf[iz, ix, il] = grow_ref[...]
-
-    block = 32
+
+    barrier = pltpu.get_barrier_semaphore()
+    peers = [to_column(k) for k in range(1, NZ * NC)]
+    peers += [to_plane(k) for k in range(1, NX * NY)]
+    peers += [to_rep(k) for k in range(1, NYH * NC) if k % NC and k // NC]
+    for dev in peers:
+        pl.semaphore_signal(barrier, inc=1, device_id=dev, device_id_type=MESH)
+
+
+    block = 64
     for t in range(parts):
         loads[t].wait()
         if t == 0:
@@ -110,6 +115,23 @@
             high = scaled.astype(BF16)
             hi[rows, :] = high
             lo[rows, :] = (scaled - high.astype(F32)).astype(BF16)
+
+    for t in range(parts + 1, parts + 4):
+        loads[t].wait()
+    wbuf[ic, iz, ix, il] = w_ref[ic]
+    own = gain_ref.shape[1]
+    spread = jnp.broadcast_to(gain_ref[...].astype(F32), (own, own))
+    r_at = lax.broadcasted_iota(jnp.int32, (own, own), 0)
+    diagonal = jnp.where(
+        r_at == lax.broadcasted_iota(jnp.int32, (own, own), 1), spread, 0.0
+    ).astype(BF16)
+    gcol = jnp.dot(diagonal, jnp.ones((own, 128), BF16), preferred_element_type=F32)
+    for cc in range(NC):
+        gcol_ref[cc] = gcol[cc * 8 : cc * 8 + 8]
+    lane = lax.broadcasted_iota(jnp.int32, (own, 128), 1) - (ix * NYL + il) * own
+    chosen = lane == lax.broadcasted_iota(jnp.int32, (own, 128), 0)
+    grow_ref[...] = jnp.sum(jnp.where(chosen, gcol, 0.0), axis=0, keepdims=True)
+    gbuf[iz, ix, il] = grow_ref[...]
 
     def group(n):
         half = (n + 1) // 2
@@ -215,6 +237,18 @@
     def _(n):
         reduce_y(n)
 
+    behind = 3
+
+    def reduce_yz(n):
+        reduce_y(n)
+        reduce_z(n - behind)
+        for zl in range(2):
+            z_copy(zl, n - behind).start()
+
+    @pl.loop(3, 6)
+    def _(n):
+        reduce_yz(n)
+
     for k in range(1, NZ):
         fz = at_z(NZ - k)
         arrived(wbuf.at[ic, fz, ix, il], wz_s.at[k - 1], wz_r.at[k - 1])
@@ -222,14 +256,9 @@
     send(wbuf.at[ic, :, ix, il], wbuf.at[ic, :, ix, il], wy_s, wy_r, {"yl": 1 - il})
     send(gbuf.at[:, ix, il], gbuf.at[:, ix, il], gy_s, gy_r, {"yl": 1 - il})
 
-    behind = 3
-
-    @pl.loop(3, NG)
-    def _(n):
-        reduce_y(n)
-        reduce_z(n - behind)
-        for zl in range(2):
-            z_copy(zl, n - behind).start()
+    @pl.loop(6, NG)
+    def _(n):
+        reduce_yz(n)
 
     arrived(wbuf.at[ic, :, ix, 1 - il], wy_s, wy_r)
     arrived(gbuf.at[:, ix, 1 - il], gy_s, gy_r)
@@ -254,23 +283,23 @@
         own = own + zr[fz]
     piece = own * gcol_ref[ic]
     gb[ih, ic] = piece
+    there = iz * NC + ic
+    sqz[there] = jnp.sum(piece * piece, axis=0, keepdims=True)
+    for k in sorted(range(1, NZ * NC), key=lambda k: -min(k // NC, NZ - k // NC)):
+        send(sqz.at[there], sqz.at[there], qz_s.at[k - 1], qz_r.at[there], to_column(k))
+    for k in range(1, NYH * NC):
+        send(gb.at[ih, ic], gb.at[ih, ic], rg_s.at[k - 1], rg_r.at[k - 1], to_rep(k))
+    for k in range(1, NZ * NC):
+        there = at_z(k // NC) * NC + lax.rem(ic + k % NC, NC)
+        arrived(sqz.at[there], qz_s.at[0], qz_r.at[there])
+    row = sqz[0]
+    for k in range(1, NZ * NC):
+        row = row + sqz[k]
+
     here = ix * NY + iy
-    sqp[here] = jnp.sum(piece * piece, axis=0, keepdims=True)
+    sqp[here] = row
     for k in sorted(range(1, NX * NY), key=lambda k: -min(k % NY, NY - k % NY)):
         send(sqp.at[here], sqp.at[here], qp_s.at[k - 1], qp_r.at[here], to_plane(k))
-    for k in range(1, NYH * NC):
-        send(gb.at[ih, ic], gb.at[ih, ic], rg_s.at[k - 1], rg_r.at[k - 1], to_rep(k))
-    for k in range(1, NX * NY):
-        there = at_x(k // NY) * NY + at_y(k % NY)
-        arrived(sqp.at[there], qp_s.at[0], qp_r.at[there])
-    row = sqp[0]
-    for k in range(1, NX * NY):
-        row = row + sqp[k]
-
-    there = iz * NC + ic
-    sqz[there] = row
-    for k in sorted(range(1, NZ * NC), key=lambda k: -min(k // NC, NZ - k // NC)):
-        send(sqz.at[there], sqz.at[there], qz_s.at[k - 1], qz_r.at[there], to_column(k))
 
     for k in (1, 3, 2):
         fx = at_x(NX - k)
@@ -317,12 +346,12 @@
     for k in range(1, NYH * NC):
         fh, fc = lax.rem(ih + NYH - k // NC, NYH), lax.rem(ic + k % NC, NC)
         arrived(gb.at[fh, fc], rg_s.at[k - 1], rg_r.at[k - 1])
-    for k in range(1, NZ * NC):
-        there = at_z(k // NC) * NC + lax.rem(ic + k % NC, NC)
-        arrived(sqz.at[there], qz_s.at[0], qz_r.at[there])
-    row = sqz[0]
-    for k in range(1, NZ * NC):
-        row = row + sqz[k]
+    for k in range(1, NX * NY):
+        there = at_x(k // NY) * NY + at_y(k % NY)
+        arrived(sqp.at[there], qp_s.at[0], qp_r.at[there])
+    row = sqp[0]
+    for k in range(1, NX * NY):
+        row = row + sqp[k]
     squares = jnp.sum(row, axis=1, keepdims=True)
     factor = 1.0 / jnp.maximum(1.0, jnp.sqrt(squares / (width * 512)))
     for hh in range(NYH):
@@ -353,12 +382,6 @@
     columns = value_grad.shape[2]
     tokens = batch * tok
     own = norm_gain.shape[0]
-    gain = norm_gain.astype(F32)
-    place = lax.axis_index("x") * NYL + lax.axis_index("yl")
-    lanes = jnp.arange(128) // own == place
-    grow = jnp.where(lanes, jnp.tile(gain, 128 // own), 0.0).reshape(1, 128)
-    gcol = jnp.broadcast_to(gain.reshape(NC, own // NC, 1), (NC, own // NC, 128))
-    weight = jnp.moveaxis(value_weight.reshape(own, NC, columns // NC), 1, 0)
     vm = pl.BlockSpec(memory_space=pltpu.VMEM)
     hbm = pl.BlockSpec(memory_space=pltpu.HBM)
     dma = pltpu.SemaphoreType.DMA
@@ -371,6 +394,10 @@
     scratch = [
         v((tokens, width), BF16),
         v((tokens, columns), BF16),
+        v((NC, own, columns // NC), BF16),
+        v((1, own), BF16),
+        v((1, 128), F32),
+        v((NC, own // NC, 128), F32),
         v((tokens, 128), F32),
         v((tokens, columns), BF16),
         v((tokens, columns), BF16),
@@ -391,26 +418,32 @@
         v((NZ, NX, NYL, 1, 128), F32),
         v((tokens, width + 128), F32),
         v((8, width), F32),
-        dma((5,)),
+        dma((8,)),
         *sem(NZ - 1), *sem(NZ - 1), *sem(), *sem(), *sem(NX - 1), *sem(NX - 1), *sem(NX),
         *sem(NG), *sem(NX - 1, NG), *sem(NY - 1, NG), dma((NG, 2)), dma((NZ,)),
         *sem(NYH * NC - 1), dma((NX * NY - 1,)), dma((NX * NY,)),
         dma((NZ * NC - 1,)), dma((NZ * NC,)),
     ]
+    operands = (
+        activations.reshape(tokens, width),
+        value_grad.reshape(tokens, columns),
+        norm_gain.reshape(1, own),
+        value_weight,
+    )
     result, update = pl.pallas_call(
         kernel,
         out_shape=(
             jax.ShapeDtypeStruct((tokens, width), BF16),
             jax.ShapeDtypeStruct((own, columns), F32),
         ),
-        in_specs=[hbm, hbm, vm, vm, vm],
+        in_specs=[hbm] * 4,
         out_specs=(vm, vm),
         scratch_shapes=scratch,
         compiler_params=pltpu.CompilerParams(
             collective_id=0, has_side_effects=True, vmem_limit_bytes=48 * 1024 * 1024
         ),
         name="normed_value_backward",
-    )(activations.reshape(tokens, width), value_grad.reshape(tokens, columns), weight, grow, gcol)
+    )(*(pltpu.with_memory_space_constraint(a, pltpu.HBM) for a in operands))
     return result.reshape(activations.shape), update
 
 

time: 74.3 us -> 68.7 us (0.925)
  local copies, waits for them, and re-layouts: 4.64 us -> 1.59 us
  Pallas kernels: 68.7 us -> 66.4 us
    unnamed x10 -> x2, local copies, waits for them, and re-layouts: 4.41 us -> 1.59 us
    pallas_call x1, Pallas kernels: 68.7 us -> 66.4 us  [on_device(): pl.pallas_call(kernel, out_shape=(jax.ShapeDtypeStruct((tokens, width), B...]
where the time goes in v3:
time: 68.7 us; the launch traced here: 68.6 us
  Pallas kernels  66.4 us (97%)
  local copies, waits for them, and re-layouts  1.59 us (2%)
    pallas_call x1, Pallas kernels, on_device(): pl.pallas_call(kernel, out_shape=(jax.ShapeDtypeStruct((tokens, width), B...  66.4 us
    unnamed x2, local copies, waits for them, and re-layouts  1.59 us

profile of v3, /device:TPU:1, one launch (start us, length us, event | category | flops | bytes accessed | tf_op | source)
XLA Modules:
  0.0 68.6 jit_solution(8279315070415737557)
XLA Ops:
  0.6 66.4 %normed_value_backward.1 = (bf16[256,2048]{1,0:T(8,128)(2,1)S(1)}, f32[16,512]{1,0:T(8,128)S(1)}) custom-call(bf16[256,2048]{1,0:T(8,128)(2,1)} %bitcast.5, bf16[256,512]{1,0:T(8,128)(2,1)} %bitcast.6, bf16[1,16]{1,0:T(2,128)(2,1)} %bitcast.7, bf16[16,512]{1,0:T(8,128)(2,1)} %w_hbm.1), custom_call_target="tpu_custom_call" | custom-call | tf_op jit(solution)/shard_map/normed_value_backward/pallas_call | solution.py:433
  67.0 1.0 %copy.8 = bf16[4,64,2048]{2,1,0:T(8,128)(2,1)} copy(bf16[4,64,2048]{2,1,0:T(8,128)(2,1)S(1)} %bitcast.4) | data formatting | bytes 2097152
  68.0 0.6 copy.9

commit v4 on v3

--- a/solution.py
+++ b/solution.py
@@ -21,7 +21,7 @@
     out_ref, upd_ref,
     x_ref, vg_ref, w_ref, gain_ref, grow_ref, gcol_ref, rstd, hi, lo, g, r, xs, xr, s, sb, yr, yb, s2, zr, gb, sqp, sqz,
     wbuf, gbuf, hbuf, gainrow,
-    ld, wz_s, wz_r, gz_s, gz_r, wy_s, wy_r, gy_s, gy_r, wx_s, wx_r, gx_s, gx_r, wc_s, wc_r,
+    ld, wz_s, wz_r, gz_s, gz_r, wy_s, wy_r, gy_s, gy_r, wx_s, wx_r, gx_s, gx_r, vx_s, vx_r, vy_s, vy_r, wc_s, wc_r,
     dc_s, dc_r, rx_s, rx_r, ry_s, ry_r, rz_s, rz_r, rg_s, rg_r, qp_s, qp_r, qz_s, qz_r,
 ):
     iz, ix, il, ih, ic = (lax.axis_index(a) for a in AXES)
@@ -253,19 +253,17 @@
         fz = at_z(NZ - k)
         arrived(wbuf.at[ic, fz, ix, il], wz_s.at[k - 1], wz_r.at[k - 1])
         arrived(gbuf.at[fz, ix, il], gz_s.at[k - 1], gz_r.at[k - 1])
-    send(wbuf.at[ic, :, ix, il], wbuf.at[ic, :, ix, il], wy_s, wy_r, {"yl": 1 - il})
+    left, right = pl.ds(0, 128), pl.ds(128, 128)
+    mine = wbuf.at[ic, :, ix, il, :, left]
+    send(mine, mine, wy_s, wy_r, {"yl": 1 - il})
+    mine = wbuf.at[ic, :, ix, il, :, right]
+    for k in (2, 1, 3):
+        send(mine, mine, wx_s.at[k - 1], wx_r.at[k - 1], to_x(k))
     send(gbuf.at[:, ix, il], gbuf.at[:, ix, il], gy_s, gy_r, {"yl": 1 - il})
 
     @pl.loop(6, NG)
     def _(n):
         reduce_yz(n)
-
-    arrived(wbuf.at[ic, :, ix, 1 - il], wy_s, wy_r)
-    arrived(gbuf.at[:, ix, 1 - il], gy_s, gy_r)
-    for k in (2, 1, 3):
-        send(wbuf.at[ic, :, ix], wbuf.at[ic, :, ix], wx_s.at[k - 1], wx_r.at[k - 1], to_x(k))
-        send(gbuf.at[:, ix], gbuf.at[:, ix], gx_s.at[k - 1], gx_r.at[k - 1], to_x(k))
-    send(wbuf.at[ic, :, ix], wbuf.at[ic, :, ix], wc_s.at[0], wc_r.at[0], sibling)
 
     @pl.loop(NG - behind, NG - 1)
     def _(n):
@@ -275,6 +273,17 @@
 
     reduce_z(NG - 1)
     z_copy(1 - parity, NG - 1).start()
+
+    arrived(wbuf.at[ic, :, ix, 1 - il, :, left], wy_s, wy_r)
+    arrived(gbuf.at[:, ix, 1 - il], gy_s, gy_r)
+    mine = wbuf.at[ic, :, ix, :, :, left]
+    for k in (2, 1, 3):
+        send(mine, mine, vx_s.at[k - 1], vx_r.at[k - 1], to_x(k))
+        send(gbuf.at[:, ix], gbuf.at[:, ix], gx_s.at[k - 1], gx_r.at[k - 1], to_x(k))
+    for k in (1, 3, 2):
+        arrived(wbuf.at[ic, :, at_x(NX - k), il, :, right], wx_s.at[k - 1], wx_r.at[k - 1])
+    mine = wbuf.at[ic, :, :, il, :, right]
+    send(mine, mine, vy_s, vy_r, {"yl": 1 - il})
 
     own = s2[NG - 1, pl.ds(pl.multiple_of(parity * 8, 8), 8), :]
     for k in sorted(range(1, NZ), key=lambda k: -min(k, NZ - k)):
@@ -303,9 +312,10 @@
 
     for k in (1, 3, 2):
         fx = at_x(NX - k)
-        arrived(wbuf.at[ic, :, fx], wx_s.at[k - 1], wx_r.at[k - 1])
+        arrived(wbuf.at[ic, :, fx, :, :, left], vx_s.at[k - 1], vx_r.at[k - 1])
         arrived(gbuf.at[:, fx], gx_s.at[k - 1], gx_r.at[k - 1])
-        send(wbuf.at[ic, :, fx], wbuf.at[ic, :, fx], wc_s.at[k], wc_r.at[k], sibling)
+    arrived(wbuf.at[ic, :, :, 1 - il, :, right], vy_s, vy_r)
+    send(wbuf.at[ic], wbuf.at[ic], wc_s, wc_r, sibling)
     for z in range(NZ):
         row = jnp.zeros((1, 128), F32)
         for xx in range(NX):
@@ -313,9 +323,7 @@
                 row = row + gbuf[z, xx, yl]
         gainrow[:, z * 128 : (z + 1) * 128] = jnp.broadcast_to(row, (8, 128))
     hbuf[:, width:] = jnp.zeros((tokens, 128), F32)
-    for k in range(NX):
-        fx = at_x(NX - k)
-        arrived(wbuf.at[oc, :, fx], wc_s.at[k], wc_r.at[k])
+    arrived(wbuf.at[oc], wc_s, wc_r)
 
     @pl.loop(0, NG)
     def _(n):
@@ -419,7 +427,8 @@
         v((tokens, width + 128), F32),
         v((8, width), F32),
         dma((8,)),
-        *sem(NZ - 1), *sem(NZ - 1), *sem(), *sem(), *sem(NX - 1), *sem(NX - 1), *sem(NX),
+        *sem(NZ - 1), *sem(NZ - 1), *sem(), *sem(), *sem(NX - 1), *sem(NX - 1),
+        *sem(NX - 1), *sem(), *sem(),
         *sem(NG), *sem(NX - 1, NG), *sem(NY - 1, NG), dma((NG, 2)), dma((NZ,)),
         *sem(NYH * NC - 1), dma((NX * NY - 1,)), dma((NX * NY,)),
         dma((NZ * NC - 1,)), dma((NZ * NC,)),

time: 68.7 us -> 68.4 us (level)
  no operation moved by 1% of the time
where the time goes in v4:
time: 68.4 us; the launch traced here: 68.2 us
  Pallas kernels  66 us (96%)
  local copies, waits for them, and re-layouts  1.59 us (2%)
    pallas_call x1, Pallas kernels, on_device(): pl.pallas_call(kernel, out_shape=(jax.ShapeDtypeStruct((tokens, width), B...  66 us
    unnamed x2, local copies, waits for them, and re-layouts  1.59 us

profile of v4, /device:TPU:1, one launch (start us, length us, event | category | flops | bytes accessed | tf_op | source)
XLA Modules:
  0.0 68.2 jit_solution(10016403152467273441)
XLA Ops:
  0.6 66.0 %normed_value_backward.1 = (bf16[256,2048]{1,0:T(8,128)(2,1)S(1)}, f32[16,512]{1,0:T(8,128)S(1)}) custom-call(bf16[256,2048]{1,0:T(8,128)(2,1)} %bitcast.5, bf16[256,512]{1,0:T(8,128)(2,1)} %bitcast.6, bf16[1,16]{1,0:T(2,128)(2,1)} %bitcast.7, bf16[16,512]{1,0:T(8,128)(2,1)} %w_hbm.1), custom_call_target="tpu_custom_call" | custom-call | tf_op jit(solution)/shard_map/normed_value_backward/pallas_call | solution.py:442
  66.6 1.0 %copy.8 = bf16[4,64,2048]{2,1,0:T(8,128)(2,1)} copy(bf16[4,64,2048]{2,1,0:T(8,128)(2,1)S(1)} %bitcast.4) | data formatting | bytes 2097152
  67.6 0.6 copy.9
